TPU v7x, 768 devices: a whole 4x8x12 slice. The times are simulated.
768 devices in a mesh: fsdp: 48 (over x, z), grp: 16 (over y, core).
Axes of the slice: x: 4, y: 8, z: 12, core: 2. Of those that a mesh axis runs over, the one named last changes fastest.
Arguments:
- gradient: bfloat16 [768, 512, 512], P('fsdp', 'grp'), may hold values from -6 to 6
- left_factor: bfloat16 [2304, 512, 512], P(('fsdp', 'grp'))
- right_factor: bfloat16 [2304, 512, 512], P(('fsdp', 'grp'))
- block_owner: int32 [768], replicated, may hold values from 0 to 767, as said below
Outputs:
- preconditioned: bfloat16 [768, 512, 512], P('fsdp', 'grp')
Inputs may be any that keep to these rules, and one draw needn't show every extreme that they name: block_owner[b] is a device index, fsdp index times 16 plus grp index. The 16 blocks homed at one fsdp index go to devices of 16 different fsdp indices; the devices of each fsdp index own 16 blocks in all; no device owns more than 3 blocks, and at every fsdp index one device owns exactly 3.
All inputs are finite; a program needn't handle non-finite values.
Results may differ from a plain program's by a relative error of at most 0.0049.
Values may be sent and summed in bfloat16 or wider, within the bound.
No kernel may reach another device: no remote copies, remote signals or barrier semaphores. Data moves between devices by JAX's collectives and lax.ppermute only.
A program may use at most 32 MiB of HBM per device.

v0:
```python
import jax
import jax.numpy as jnp
from jax import lax
from jax.sharding import Mesh
from jax.sharding import PartitionSpec as P

GRP = ("grp_0", "grp_1")
FSDP_GRP = ("fsdp", "grp_0", "grp_1")


def in_blocks(shard, dim, size):
    before, after = (shard.shape[:dim], shard.shape[dim + 1 :])
    return jnp.moveaxis(shard.reshape(*before, size, -1, *after), dim, 0)


def joined_along(pieces, dim):
    dims = list(pieces.shape[1:])
    dims[dim] *= pieces.shape[0]
    return jnp.moveaxis(pieces, 0, dim).reshape(dims)


def turned_blocks(pieces, axes, sequence):
    dims = [lax.axis_size(a) for a in axes]
    pieces = pieces.reshape(*dims, *pieces.shape[1:])
    for k in sequence:
        pieces = lax.all_to_all(pieces, axes[k], split_axis=k, concat_axis=k, tiled=True)
    return pieces.reshape(-1, *pieces.shape[len(axes) :])


def core_and_chips(shard, groups, sequence, split_dim, concat_dim):
    size = lax.axis_size(groups[0]) * lax.axis_size(groups[1])
    pieces = in_blocks(shard, split_dim, size)
    return joined_along(turned_blocks(pieces, groups, sequence), concat_dim)


def per_device(gradient, left_factor, right_factor, block_owner):
    local_blocks = gradient.shape[0]
    piece_rows = gradient.shape[1]
    block_width = gradient.shape[2]
    slot_count = left_factor.shape[0]
    columns = lax.axis_size("fsdp")
    groups = lax.axis_size(GRP)
    column = lax.axis_index("fsdp")
    owners_all = block_owner.reshape(columns, local_blocks)
    dest_column = owners_all // groups
    dest_group = owners_all % groups
    mine_column = lax.dynamic_index_in_dim(dest_column, column, 0, keepdims=False)
    column_ids = jnp.arange(columns, dtype=jnp.int32)
    matching = mine_column[None, :] == column_ids[:, None]
    pick_send = matching.astype(jnp.bfloat16)
    outgoing = jnp.einsum(
        "cj,jrd->crd", pick_send, gradient, preferred_element_type=jnp.float32
    ).astype(jnp.bfloat16)
    arrived = lax.all_to_all(
        outgoing.reshape(columns * piece_rows, block_width),
        "fsdp",
        split_axis=0,
        concat_axis=0,
        tiled=True,
    )
    arrived = arrived.reshape(columns, piece_rows, block_width)
    toward = dest_column == column
    live_source = jnp.sum(toward.astype(jnp.int32), axis=1) > 0
    target = jnp.sum(jnp.where(toward, dest_group, 0), axis=1)
    same_owner = (target[None, :] == target[:, None]) & live_source[None, :] & live_source[:, None]
    before = column_ids[None, :] < column_ids[:, None]
    rank_slot = jnp.sum((same_owner & before).astype(jnp.int32), axis=1)
    group_ids = jnp.arange(groups, dtype=jnp.int32)
    slot_ids = jnp.arange(slot_count, dtype=jnp.int32)
    routing = (
        live_source[None, None, :]
        & (target[None, None, :] == group_ids[:, None, None])
        & (rank_slot[None, None, :] == slot_ids[None, :, None])
    )
    routing = routing.astype(jnp.bfloat16)
    packed = jnp.einsum(
        "oks,srd->kord", routing, arrived, preferred_element_type=jnp.float32
    ).astype(jnp.bfloat16)
    packed = packed.reshape(slot_count, groups * piece_rows, block_width)
    blocks = lax.all_to_all(packed, GRP, split_axis=1, concat_axis=1, tiled=True)
    left_product = jnp.einsum(
        "kab,kbc->kac", left_factor, blocks, preferred_element_type=jnp.float32
    ).astype(jnp.bfloat16)
    result = jnp.einsum(
        "kab,kbc->kac", left_product, right_factor, preferred_element_type=jnp.float32
    ).astype(jnp.bfloat16)
    returned = core_and_chips(result, ("grp_0", "grp_1"), (1, 0), 1, 1)
    returned = returned.reshape(slot_count, groups, piece_rows, block_width)
    unpacked = jnp.einsum(
        "oks,kord->srd", routing, returned, preferred_element_type=jnp.float32
    ).astype(jnp.bfloat16)
    homeward = lax.all_to_all(
        unpacked.reshape(columns * piece_rows, block_width),
        "fsdp",
        split_axis=0,
        concat_axis=0,
        tiled=True,
    )
    homeward = homeward.reshape(columns, piece_rows, block_width)
    return jnp.einsum(
        "cj,crd->jrd", pick_send, homeward, preferred_element_type=jnp.float32
    ).astype(jnp.bfloat16)


def solution(mesh):
    finer = Mesh(mesh.devices.reshape(mesh.shape["fsdp"], 8, 2), ("fsdp", "grp_0", "grp_1"))
    placed = (P("fsdp", GRP, None), P(FSDP_GRP, None, None), P(FSDP_GRP, None, None), P())
    return jax.shard_map(
        per_device, mesh=finer, in_specs=placed, out_specs=P("fsdp", GRP, None), check_vma=False
    )
```

profile of v0, /device:TPU:6, one launch (start us, length us, event | category | flops | bytes accessed | tf_op | source)
XLA Modules:
  0.0 268.5 jit_solution(4873936425791648194)
XLA Ops:
  0.0 0.0 copy-start
  0.0 0.9 reshape.100
  0.9 1.7 convolution_convert_fusion.1
  2.7 2.0 copy.35
  4.7 18.5 %all-to-all-start = ((bf16[48,32,512]{2,1,0:T(8,128)(2,1)}), bf16[48,32,512]{2,1,0:T(8,128)(2,1)S(1)}, u32[]{:S(2)}, u32[]{:S(2)}) async-start(bf16[48,32,512]{2,1,0:T(8,128)(2,1)} %copy.35), calls=%async_computation | async-start | bytes 3145728 | tf_op jit(solution)/shard_map/all_to_all | solution.py:54
  23.2 0.1 convert_reduce_fusion.1
  23.4 0.2 convert_reduce_fusion
  23.6 58.2 %all-to-all-done = bf16[48,32,512]{2,1,0:T(8,128)(2,1)S(1)} async-done(((bf16[48,32,512]{2,1,0:T(8,128)(2,1)}), bf16[48,32,512]{2,1,0:T(8,128)(2,1)S(1)}, u32[]{:S(2)}, u32[]{:S(2)}) %all-to-all-start) | async-done | bytes 1572896 | tf_op jit(solution)/shard_map/all_to_all | solution.py:54
  81.7 1.4 fusion.5
  83.1 0.9 copy.37
  84.0 1.4 copy.38
  85.3 56.8 %all_to_all.27 = bf16[3,512,512]{2,0,1:T(4,128)(2,1)} all-to-all(bf16[3,512,512]{2,0,1:T(4,128)(2,1)S(1)} %copy.38), channel_id=1, replica_groups=mesh['fsdp'=48,'grp_0'=8,'grp_1'=2] {'grp_0','grp_1'}, dimensions={1} | all-to-all | bytes 3145728 | tf_op jit(solution)/shard_map/all_to_all | solution.py:80
  142.1 0.0 copy-done
  142.1 4.2 %convolution_convert_fusion.2 = bf16[3,512,512]{2,1,0:T(8,128)(2,1)S(1)} fusion(bf16[3,512,512]{2,1,0:T(8,128)(2,1)S(1)} %copy-done, bf16[3,512,512]{2,1,0:T(8,128)(2,1)} %param.5, bf16[3,512,512]{2,0,1:T(4,128)(2,1)} %all_to_all.27), kind=kOutput, calls=%fused_computation.3 | convolution fusion | flops 1612185600 | bytes 6291456 | tf_op jit(solution)/shard_map/kab,kbc->kac/dot_general | solution.py:84
  146.3 0.1 copy.42
  146.4 6.2 %all_to_all.28 = bf16[8,2,3,32,512]{4,3,0,2,1:T(8,128)(2,1)S(1)} all-to-all(bf16[8,2,3,32,512]{4,3,0,2,1:T(8,128)(2,1)S(1)} %copy.42), channel_id=1, replica_groups=mesh['fsdp'=48,'grp_0'=8,'grp_1'=2] {'grp_1'}, dimensions={1} | all-to-all | bytes 3145728 | tf_op jit(solution)/shard_map/all_to_all | solution.py:26
  152.6 0.2 copy.43
  152.8 43.0 %all_to_all.29 = bf16[8,2,3,32,512]{4,3,1,2,0:T(8,128)(2,1)S(1)} all-to-all(bf16[8,2,3,32,512]{4,3,1,2,0:T(8,128)(2,1)S(1)} %copy.43), channel_id=1, replica_groups=mesh['fsdp'=48,'grp_0'=8,'grp_1'=2] {'grp_0'}, dimensions={0} | all-to-all | bytes 3145728 | tf_op jit(solution)/shard_map/all_to_all | solution.py:26
  195.8 2.8 %copy.44 = bf16[8,2,3,32,512]{4,1,0,2,3:T(2,128)(2,1)} copy(bf16[8,2,3,32,512]{4,3,1,2,0:T(8,128)(2,1)S(1)} %all_to_all.29) | data formatting | bytes 3145728 | tf_op jit(solution)/shard_map/all_to_all | solution.py:26
  198.6 2.5 reshape.104
  201.1 0.6 bitcast_convert_fusion
  201.7 0.9 copy.45
  202.6 63.8 %all_to_all.30 = bf16[48,32,512]{2,1,0:T(8,128)(2,1)S(1)} all-to-all(bf16[48,32,512]{2,1,0:T(8,128)(2,1)S(1)} %copy.45), channel_id=1, replica_groups=mesh['fsdp'=48,'grp_0'=8,'grp_1'=2] {'fsdp'}, dimensions={0} | all-to-all | bytes 3145728 | tf_op jit(solution)/shard_map/all_to_all | solution.py:92
  266.4 1.0 fusion.8
  267.4 1.1 copy.47
  (5 shorter events, 0.1 us)
Async XLA Ops:
  0.0 142.1 %copy-start = (bf16[3,512,512]{2,1,0:T(8,128)(2,1)S(1)}, bf16[3,512,512]{2,1,0:T(8,128)(2,1)}, u32[]{:S(2)}) copy-start(bf16[3,512,512]{2,1,0:T(8,128)(2,1)} %param.6) | copy-start | bytes 4718596
  4.7 77.0 %all-to-all-start = ((bf16[48,32,512]{2,1,0:T(8,128)(2,1)}), bf16[48,32,512]{2,1,0:T(8,128)(2,1)S(1)}, u32[]{:S(2)}, u32[]{:S(2)}) async-start(bf16[48,32,512]{2,1,0:T(8,128)(2,1)} %copy.35), calls=%async_computation | async-start | bytes 3145728 | tf_op jit(solution)/shard_map/all_to_all | solution.py:54
where the time goes:
time: 269 us
  blocking collectives  170 us (63%)
  waiting for transfers between devices  58.2 us (22%)
  starting transfers between devices  18.5 us (7%)
  local copies, waits for them, and re-layouts  12.6 us (5%)
  matrix products  8.95 us (3%)
    all_to_all x1, blocking collectives, per_device(): lax.all_to_all(unpacked.reshape(columns * piece_rows, block_width), 'fsdp...  63.8 us
    all_to_all x1, waiting for transfers between devices, per_device(): lax.all_to_all(outgoing.reshape(columns * piece_rows, block_width), 'fsdp...  58.2 us
    all_to_all x1, blocking collectives, per_device(): lax.all_to_all(packed, GRP, split_axis=1, concat_axis=1, tiled=True)  56.8 us
    all_to_all x2, blocking collectives, turned_blocks(): lax.all_to_all(pieces, axes[k], split_axis=k, concat_axis=k, tiled=True)  49.2 us
    all_to_all x1, starting transfers between devices, per_device(): lax.all_to_all(outgoing.reshape(columns * piece_rows, block_width), 'fsdp...  18.5 us
  transfers between devices with their start and end apart: 1, of which 1 were waited for; matrix products, arithmetic and copies ran while one was open for 0% of the time, Pallas kernels for 0%

commit v1 on v0

v1 whole, which is shorter than its diff:
```python
import jax
import jax.numpy as jnp
from jax import lax
from jax.experimental import pallas as pl
from jax.experimental.pallas import tpu as pltpu
from jax.sharding import PartitionSpec as P

VMEM = pltpu.VMEM
SMEM = pltpu.SMEM


def place_kernel(table, source, out):
    for i in range(source.shape[0]):
        out[table[i]] = source[i]


def place_live_kernel(table, source, out):
    def step(i, carry):
        @pl.when(table[i] >= 0)
        def _():
            out[table[i]] = source[i]

        return carry

    lax.fori_loop(0, source.shape[0], step, 0)


def fetch_live_kernel(table, source, out):
    def step(i, carry):
        @pl.when(table[i] >= 0)
        def _():
            out[i] = source[table[i]]

        return carry

    lax.fori_loop(0, out.shape[0], step, 0)


def fetch_kernel(table, source, out):
    for i in range(out.shape[0]):
        out[i] = source[table[i]]


def moved(kernel, table, source, pieces, name, resident=True):
    if resident:
        source = pltpu.with_memory_space_constraint(source, VMEM)
    return pl.pallas_call(
        kernel,
        out_shape=VMEM((pieces, *source.shape[1:]), source.dtype),
        in_specs=[pl.BlockSpec(memory_space=SMEM), pl.BlockSpec(memory_space=VMEM)],
        out_specs=pl.BlockSpec(memory_space=VMEM),
        name=name,
        compiler_params=pltpu.CompilerParams(vmem_limit_bytes=4 << 20),
    )(table, source)


def product_kernel(left, blocks, right, out):
    slots, size, _ = left.shape
    for k in range(slots):
        block = blocks[:, k].reshape(size, size)
        half = jnp.dot(left[k], block, preferred_element_type=jnp.float32).astype(left.dtype)
        full = jnp.dot(half, right[k], preferred_element_type=jnp.float32).astype(left.dtype)
        out[:, k] = full.reshape(out.shape[0], *out.shape[2:])


def products(left, blocks, right):
    slots, size, _ = left.shape
    resident = pl.BlockSpec(memory_space=VMEM)
    return pl.pallas_call(
        product_kernel,
        out_shape=VMEM(blocks.shape, blocks.dtype),
        in_specs=[resident, resident, resident],
        out_specs=resident,
        name="products",
        compiler_params=pltpu.CompilerParams(vmem_limit_bytes=16 << 20),
        cost_estimate=pl.CostEstimate(
            flops=4 * slots * size**3, transcendentals=0, bytes_accessed=2 * (2 * left.size + 2 * blocks.size)
        ),
    )(*(pltpu.with_memory_space_constraint(x, VMEM) for x in (left, blocks, right)))


def exchanged(pieces, axis):
    return lax.all_to_all(pieces, axis, split_axis=0, concat_axis=0, tiled=True)


def per_device(gradient, left_factor, right_factor, block_owner):
    local_blocks, rows, width = gradient.shape
    slots = left_factor.shape[0]
    columns = lax.axis_size("fsdp")
    groups = lax.axis_size("grp")
    column = lax.axis_index("fsdp")
    mine = lax.dynamic_slice_in_dim(block_owner, column * local_blocks, local_blocks) // groups
    outgoing = moved(place_kernel, mine, gradient, columns, "to_columns", False)
    arrived = exchanged(outgoing, "fsdp")
    owners = block_owner.reshape(columns, local_blocks)
    toward = owners // groups == column
    live = jnp.any(toward, axis=1)
    target = jnp.sum(jnp.where(toward, owners % groups, 0), axis=1)
    ids = jnp.arange(columns, dtype=jnp.int32)
    earlier = (target[None, :] == target[:, None]) & live[None, :] & (ids[None, :] < ids[:, None])
    rank = jnp.sum(earlier.astype(jnp.int32), axis=1)
    slot = jnp.where(live, target * slots + rank, -1).astype(jnp.int32)
    packed = moved(place_live_kernel, slot, arrived, groups * slots, "to_slots")
    blocks = exchanged(packed.reshape(groups, slots, rows, width), "grp")
    result = products(left_factor, blocks, right_factor)
    returned = exchanged(result, "grp").reshape(groups * slots, rows, width)
    homeward = moved(fetch_live_kernel, slot, returned, columns, "from_slots")
    home = exchanged(homeward, "fsdp")
    return moved(fetch_kernel, mine, home, local_blocks, "from_columns")


def solution(mesh):
    placed = (P("fsdp", "grp", None), P(("fsdp", "grp"), None, None), P(("fsdp", "grp"), None, None), P())
    return jax.shard_map(
        per_device, mesh=mesh, in_specs=placed, out_specs=P("fsdp", "grp", None), check_vma=False
    )
```

time: 269 us -> 242 us (0.90); the launches traced: 269 us -> 238 us
  blocking collectives: 170 us -> 152 us
  local copies, waits for them, and re-layouts: 12.6 us -> 1.93 us
  matrix products: 8.95 us -> 0 us
  Pallas kernels: 0 us -> 6.58 us
    all_to_all x4 -> x3, blocking collectives: 170 us -> 152 us  [exchanged(): return lax.all_to_all(pieces, axis, split_axis=0, concat_axis=0, tiled=True)]
    dot_general x5 -> x0, matrix products: 8.95 us -> none  [the longest x1 4.21 us: per_device(): jnp.einsum('kab,kbc->kac', left_product, right_factor, preferred_element_...]
    pallas_call x0 -> x5, Pallas kernels: none -> 6.58 us  [the longest x4 4.78 us: moved(): pl.pallas_call(kernel, out_shape=VMEM((pieces, *source.shape[1:]), source...]
    convert_element_type x4 -> x0, local copies, waits for them, and re-layouts: 4.84 us -> none  [the longest x1 2.02 us: per_device(): outgoing = jnp.einsum('cj,jrd->crd', pick_send, gradient, preferred_eleme...]
    reshape x4 -> x1, local copies, waits for them, and re-layouts: 4.83 us -> 0.07 us  [per_device(): owners = block_owner.reshape(columns, local_blocks)]
    all_to_all x2 -> x0, local copies, waits for them, and re-layouts: 2.95 us -> none  [turned_blocks(): lax.all_to_all(pieces, axes[k], split_axis=k, concat_axis=k, tiled=True)]
where the time goes in v1:
time: 242 us; the launch traced here: 238 us
  blocking collectives  152 us (63%)
  waiting for transfers between devices  58 us (24%)
  starting transfers between devices  18.7 us (8%)
  Pallas kernels  6.58 us (3%)
    all_to_all x3, blocking collectives, exchanged(): return lax.all_to_all(pieces, axis, split_axis=0, concat_axis=0, tiled=True)  152 us
    all_to_all x1, waiting for transfers between devices, exchanged(): return lax.all_to_all(pieces, axis, split_axis=0, concat_axis=0, tiled=True)  58 us
    all_to_all x1, starting transfers between devices, exchanged(): return lax.all_to_all(pieces, axis, split_axis=0, concat_axis=0, tiled=True)  18.7 us
  transfers between devices with their start and end apart: 1, of which 1 were waited for; matrix products, arithmetic and copies ran while one was open for 0% of the time, Pallas kernels for 0%

profile of v1, /device:TPU:6, one launch (start us, length us, event | category | flops | bytes accessed | tf_op | source)
XLA Modules:
  0.0 238.5 jit_solution(6542782521190243365)
XLA Ops:
  0.0 0.8 and_select_fusion.table
  0.8 0.0 copy-start.2
  0.8 1.0 copy-done.2
  1.8 1.7 to_columns.1
  3.5 0.0 copy-start.3
  3.5 18.7 %all-to-all-start = ((bf16[48,32,512]{2,1,0:T(8,128)(2,1)}), bf16[48,32,512]{2,1,0:T(8,128)(2,1)S(1)}, u32[]{:S(2)}, u32[]{:S(2)}) async-start(bf16[48,32,512]{2,1,0:T(8,128)(2,1)} %to_columns.1), calls=%async_computation | async-start | bytes 3145728 | tf_op jit(solution)/shard_map/all_to_all | solution.py:83
  22.2 0.0 copy-done.3
  22.2 0.1 reshape.12
  22.3 0.1 fusion.2
  22.4 0.1 reduce_or.9
  22.6 0.2 convert_reduce_fusion
  22.8 58.0 %all-to-all-done.source = bf16[48,32,512]{2,1,0:T(8,128)(2,1)S(1)} async-done(((bf16[48,32,512]{2,1,0:T(8,128)(2,1)}), bf16[48,32,512]{2,1,0:T(8,128)(2,1)S(1)}, u32[]{:S(2)}, u32[]{:S(2)}) %all-to-all-start) | async-done | bytes 1572896 | tf_op jit(solution)/shard_map/all_to_all | solution.py:83
  80.7 1.2 to_slots.1
  82.0 0.0 copy-start
  82.0 0.0 copy-start.1
  82.0 45.7 %all_to_all.20.blocks = bf16[16,3,32,512]{3,2,1,0:T(8,128)(2,1)S(1)} all-to-all(bf16[16,3,32,512]{3,2,1,0:T(8,128)(2,1)S(1)} %bitcast.3), channel_id=1, replica_groups=mesh['fsdp'=48,'grp'=16] {'grp'}, dimensions={0} | all-to-all | bytes 3145728 | tf_op jit(solution)/shard_map/all_to_all | solution.py:83
  127.7 0.0 copy-done
  127.7 0.0 copy-done.1
  127.7 1.8 products.1
  129.5 42.5 %all_to_all.21 = bf16[16,3,32,512]{3,2,1,0:T(8,128)(2,1)S(1)} all-to-all(bf16[16,3,32,512]{3,2,1,0:T(8,128)(2,1)S(1)} %products.1), channel_id=1, replica_groups=mesh['fsdp'=48,'grp'=16] {'grp'}, dimensions={0} | all-to-all | bytes 3145728 | tf_op jit(solution)/shard_map/all_to_all | solution.py:83
  171.9 1.2 from_slots.1
  173.2 63.9 %all_to_all.22.source = bf16[48,32,512]{2,1,0:T(8,128)(2,1)S(1)} all-to-all(bf16[48,32,512]{2,1,0:T(8,128)(2,1)S(1)} %from_slots.1), channel_id=1, replica_groups=mesh['fsdp'=48,'grp'=16] {'fsdp'}, dimensions={0} | all-to-all | bytes 3145728 | tf_op jit(solution)/shard_map/all_to_all | solution.py:83
  237.1 0.6 from_columns.1
  237.7 0.8 copy.5
  (1 shorter events, 0.0 us)
Async XLA Ops:
  0.8 1.0 copy-start.2
  3.5 18.7 %copy-start.3 = (s32[768]{0:T(1024)S(1)}, s32[768]{0:T(1024)}, u32[]{:S(2)}) copy-start(s32[768]{0:T(1024)} %param.7) | copy-start | bytes 9220
  3.5 77.2 %all-to-all-start = ((bf16[48,32,512]{2,1,0:T(8,128)(2,1)}), bf16[48,32,512]{2,1,0:T(8,128)(2,1)S(1)}, u32[]{:S(2)}, u32[]{:S(2)}) async-start(bf16[48,32,512]{2,1,0:T(8,128)(2,1)} %to_columns.1), calls=%async_computation | async-start | bytes 3145728 | tf_op jit(solution)/shard_map/all_to_all | solution.py:83
  82.0 45.7 %copy-start = (bf16[3,512,512]{2,1,0:T(8,128)(2,1)S(1)}, bf16[3,512,512]{2,1,0:T(8,128)(2,1)}, u32[]{:S(2)}) copy-start(bf16[3,512,512]{2,1,0:T(8,128)(2,1)} %left.1) | copy-start | bytes 4718596
  82.0 45.7 %copy-start.1 = (bf16[3,512,512]{2,1,0:T(8,128)(2,1)S(1)}, bf16[3,512,512]{2,1,0:T(8,128)(2,1)}, u32[]{:S(2)}) copy-start(bf16[3,512,512]{2,1,0:T(8,128)(2,1)} %right.1) | copy-start | bytes 4718596
